TPU v7x, 32 devices: a whole 2x2x4 slice. The times are simulated.
32 devices in a mesh: pq: 8 (over z, x), hh: 4 (over y, core).
Axes of the slice: x: 2, y: 2, z: 4, core: 2. Of those that a mesh axis runs over, the one named last changes fastest.
Arguments:
- amplitudes: bfloat16 [4096, 2048], P('hh', 'pq'), may hold values from -6 to 6
- integrals: bfloat16 [4096, 2048], P('hh', 'pq'), may hold values from -0.001953125 to 0.001953125
- left_amps: bfloat16 [8, 4096, 1024], P(None, 'hh', 'pq'), may hold values from -6 to 6
Outputs:
- sigma_ladder: bfloat16 [8, 4096, 1024], P(None, 'hh', 'pq')
- subspace: float32 [8, 8], replicated
All inputs are finite; a program needn't handle non-finite values.
Results may differ from a plain program's by a relative error of at most 0.0049.
Values may be sent and summed in bfloat16 or wider, within the bound.
No kernel may reach another device: no remote copies, remote signals or barrier semaphores. Data moves between devices by JAX's collectives and lax.ppermute only.
A program may use at most 64 MiB of HBM per device.

v0:
```python
import math
import jax
import jax.numpy as jnp
from jax import lax
from jax.sharding import PartitionSpec as P

OCC_PAIRS = 4096


def body(amplitudes, integrals, left_amps):
    root_count = left_amps.shape[0]
    ab_cols = left_amps.shape[2]
    partial_t = lax.dot_general(
        integrals,
        lax.all_gather(amplitudes, "hh", axis=0, tiled=True),
        (((1,), (1,)), ((), ())),
        preferred_element_type=jnp.float32,
    )
    ladder_t = lax.psum_scatter(partial_t, "pq", scatter_dimension=1, tiled=True).astype(
        jnp.bfloat16
    )
    ladder_t = lax.all_gather(ladder_t, "pq", axis=1, tiled=True)
    rows_out = lax.dot_general(
        ladder_t,
        lax.all_gather(left_amps, "hh", axis=1, tiled=True),
        (((1,), (1,)), ((), ())),
        preferred_element_type=jnp.float32,
    )
    sigma_out = jnp.transpose(rows_out, (1, 0, 2)).astype(jnp.bfloat16)
    local_gram = jnp.dot(
        left_amps.reshape(root_count, -1),
        sigma_out.reshape(root_count, -1).T,
        preferred_element_type=jnp.float32,
    )
    factor = 1.0 / math.sqrt(OCC_PAIRS * ab_cols * lax.axis_size("pq"))
    subspace = lax.psum(local_gram, ("pq", "hh")) * factor
    return (sigma_out, subspace)


def solution(mesh):
    return jax.shard_map(
        body,
        mesh=mesh,
        in_specs=(P("hh", "pq"), P("hh", "pq"), P(None, "hh", "pq")),
        out_specs=(P(None, "hh", "pq"), P()),
        check_vma=False,
    )
```

profile of v0, /device:TPU:10, one launch (start us, length us, event | category | flops | bytes accessed | tf_op | source)
XLA Modules:
  0.0 574.5 jit_solution(7617182189609885000)
XLA Ops:
  7.2 0.0 copy-start
  7.2 0.0 all-gather.4.cloned.1.call-start
  7.2 0.7 all-gather.4.cloned.1.call-update
  7.9 0.0 reduce-scatter.2.cloned.1.call-start
  8.0 25.3 %all-gather.4.cloned.1.call-done = bf16[4096,256]{1,0:T(8,128)(2,1)} async-done(((bf16[1024,256]{1,0:T(8,128)(2,1)}), bf16[4096,256]{1,0:T(8,128)(2,1)}) %all-gather.4.cloned.1.call-update) | async-done | bytes 2097168 | tf_op jit(solution)/shard_map/all_gather | solution.py:15
  33.3 0.0 copy-done
  33.3 9.7 %fusion.12 = f32[1024,4096]{1,0:T(8,128)} fusion(bf16[1024,256]{1,0:T(8,128)(2,1)S(1)} %copy-done, bf16[4096,256]{1,0:T(8,128)(2,1)} %all-gather.4.cloned.1.call-done), kind=kOutput, calls=%fused_computation.8 | convolution fusion | flops 2147483648 | bytes 19398656 | tf_op jit(solution)/shard_map/dot_general | solution.py:13
  43.0 0.0 reduce-scatter.2.cloned.1.call-update
  43.0 0.0 all-gather.8.cloned.1.call-start
  43.1 0.7 all-gather.8.cloned.1.call-update
  43.7 0.0 all-gather.6.cloned.1.call-start
  43.8 278.5 %reduce-scatter.2.cloned.1.call-done = f32[1024,512]{1,0:T(8,128)} async-done(((f32[1024,4096]{1,0:T(8,128)}), f32[1024,512]{1,0:T(8,128)}) %reduce-scatter.2.cloned.1.call-update) | async-done | bytes 2097168 | tf_op jit(solution)/shard_map/reduce_scatter | solution.py:19
  322.3 2.7 convert_element_type.9
  325.0 0.0 all-gather.6.cloned.1.call-update
  325.1 0.0 copy-start.1
  325.1 57.3 %all-gather.8.cloned.1.call-done = bf16[8,4096,128]{2,1,0:T(8,128)(2,1)} async-done(((bf16[8,1024,128]{2,1,0:T(8,128)(2,1)}), bf16[8,4096,128]{2,1,0:T(8,128)(2,1)}) %all-gather.8.cloned.1.call-update) | async-done | bytes 8388624 | tf_op jit(solution)/shard_map/all_gather | solution.py:25
  382.3 124.7 %all-gather.6.cloned.1.call-done = bf16[1024,4096]{1,0:T(8,128)(2,1)} async-done(((bf16[1024,512]{1,0:T(8,128)(2,1)}), bf16[1024,4096]{1,0:T(8,128)(2,1)}) %all-gather.6.cloned.1.call-update) | async-done | bytes 8388624 | tf_op jit(solution)/shard_map/all_gather | solution.py:22
  507.0 13.7 %convert_bitcast_fusion = bf16[8,1024,128]{2,1,0:T(8,128)(2,1)S(1)} fusion(bf16[8,4096,128]{2,1,0:T(8,128)(2,1)} %all-gather.8.cloned.1.call-done, bf16[1024,4096]{1,0:T(8,128)(2,1)} %all-gather.6.cloned.1.call-done), kind=kOutput, calls=%fused_computation.5 | convolution fusion | flops 8590983168 | bytes 18874368 | tf_op jit(solution)/shard_map/dot_general | solution.py:23
  520.7 0.0 copy-start.2
  520.7 1.3 copy-done.2
  522.0 0.0 copy-done.1
  522.0 2.5 fusion.7
  524.5 42.8 %psum.7 = f32[8,8]{0,1:T(8,128)S(1)} all-reduce(f32[8,8]{0,1:T(8,128)S(1)} %fusion.7), channel_id=1, replica_groups=mesh['pq'=8,'hh'=4] {'pq','hh'}, use_global_device_ids=true, to_apply=%region_1.0 | all-reduce | flops 64 | bytes 512 | tf_op jit(solution)/shard_map/psum | solution.py:36
  567.3 0.7 copy.7
  (1 shorter events, 0.0 us)
Async XLA Ops:
  7.2 26.1 %copy-start = (bf16[1024,256]{1,0:T(8,128)(2,1)S(1)}, bf16[1024,256]{1,0:T(8,128)(2,1)}, u32[]{:S(2)}) copy-start(bf16[1024,256]{1,0:T(8,128)(2,1)} %param.4) | copy-start | bytes 1572868
  7.2 26.1 %all-gather.4.cloned.1.call-start = ((), (), s32[]{:S(2)}) async-start(), calls=%async_computation.1 | async-start | bytes 2621440 | tf_op jit(solution)/shard_map/all_gather | solution.py:15
  7.9 314.4 %reduce-scatter.2.cloned.1.call-start = ((), (), s32[]{:S(2)}) async-start(), calls=%async_computation.2 | async-start | bytes 18874368 | tf_op jit(solution)/shard_map/reduce_scatter | solution.py:19
  43.0 339.3 %all-gather.8.cloned.1.call-start = ((), (), s32[]{:S(2)}) async-start(), calls=%async_computation.4 | async-start | bytes 10485760 | tf_op jit(solution)/shard_map/all_gather | solution.py:25
  43.7 463.3 %all-gather.6.cloned.1.call-start = ((), (), s32[]{:S(2)}) async-start(), calls=%async_computation.3 | async-start | bytes 9437184 | tf_op jit(solution)/shard_map/all_gather | solution.py:22
  325.1 196.9 %copy-start.1 = (bf16[8,1024,128]{2,1,0:T(8,128)(2,1)S(1)}, bf16[8,1024,128]{2,1,0:T(8,128)(2,1)}, u32[]{:S(2)}) copy-start(bf16[8,1024,128]{2,1,0:T(8,128)(2,1)} %param.5) | copy-start | bytes 6291460
  520.7 1.3 copy-start.2
Sparse Core Ops, SparseCore 0:
  9.5 23.6 all-gather.3
  43.1 279.1 reduce-scatter.1
  323.9 58.3 all-gather.7
  384.8 122.1 all-gather.5
where the time goes:
time: 575 us; the launch traced here: 574 us
  waiting for transfers between devices  487 us (85%)
  blocking collectives  42.8 us (7%)
  matrix products  25.9 us (5%)
  between operations  13.8 us (2%)
    reduce_scatter x1, waiting for transfers between devices, body(): lax.psum_scatter(partial_t, 'pq', scatter_dimension=1, tiled=True)  279 us
    all_gather x1, waiting for transfers between devices, body(): ladder_t = lax.all_gather(ladder_t, 'pq', axis=1, tiled=True)  125 us
    all_gather x1, waiting for transfers between devices, body(): lax.all_gather(left_amps, 'hh', axis=1, tiled=True)  57.3 us
    psum x1, blocking collectives, body(): subspace = lax.psum(local_gram, ('pq', 'hh')) * factor  42.8 us
    all_gather x1, waiting for transfers between devices, body(): lax.all_gather(amplitudes, 'hh', axis=0, tiled=True)  25.3 us
    dot_general x1, matrix products, body(): lax.dot_general(ladder_t, lax.all_gather(left_amps, 'hh', axis=1, tiled=T...  13.7 us
  transfers between devices with their start and end apart: 4, of which 4 were waited for; matrix products, arithmetic and copies ran while one was open for 0% of the time, Pallas kernels for 0%

commit v1 on v0

--- a/solution.py
+++ b/solution.py
@@ -19,7 +19,12 @@
     ladder_t = lax.psum_scatter(partial_t, "pq", scatter_dimension=1, tiled=True).astype(
         jnp.bfloat16
     )
-    ladder_t = lax.all_gather(ladder_t, "pq", axis=1, tiled=True)
+    ring = [ladder_t]
+    for hop in range(7):
+        ring.append(lax.ppermute(ring[-1], "pq", [(dev, (dev + 1) % 8) for dev in range(8)]))
+    ladder_t = jnp.roll(
+        jnp.concatenate(ring[::-1], axis=1), (lax.axis_index("pq") + 1) * ring[0].shape[1], axis=1
+    )
     rows_out = lax.dot_general(
         ladder_t,
         lax.all_gather(left_amps, "hh", axis=1, tiled=True),

time: 575 us -> 597 us (1.038)
  waiting for transfers between devices: 487 us -> 450 us
  local copies, waits for them, and re-layouts: 1.99 us -> 33.1 us
  starting transfers between devices: 0.16 us -> 19.9 us
  blocking collectives: 42.8 us -> 48.9 us
    ppermute x0 -> x7, waiting for transfers between devices: none -> 145 us  [body(): lax.ppermute(ring[-1], 'pq', [(dev, (dev + 1) % 8) for dev in range(8)])]
    all_gather x1 -> x0, waiting for transfers between devices: 125 us -> none  [body(): ladder_t = lax.all_gather(ladder_t, 'pq', axis=1, tiled=True)]
    all_gather x1, waiting for transfers between devices: 57.3 us -> 0.01 us  [body(): lax.all_gather(left_amps, 'hh', axis=1, tiled=True)]
    unnamed x7 -> x43, local copies, waits for them, and re-layouts: 1.99 us -> 33.1 us
    ppermute x0 -> x7, starting transfers between devices: none -> 19.7 us  [body(): lax.ppermute(ring[-1], 'pq', [(dev, (dev + 1) % 8) for dev in range(8)])]
    psum x1, blocking collectives: 42.8 us -> 48.9 us  [body(): subspace = lax.psum(local_gram, ('pq', 'hh')) * factor]
  transfers between devices with their start and end apart: 4 -> 10, of which waited for: 4 -> 9; matrix products, arithmetic and copies ran while one was open for 0% -> 5% of each run, Pallas kernels for 0% -> 0%
where the time goes in v1:
time: 597 us; the launch traced here: 596 us
  waiting for transfers between devices  450 us (75%)
  blocking collectives  48.9 us (8%)
  local copies, waits for them, and re-layouts  33.1 us (6%)
  matrix products  26 us (4%)
  starting transfers between devices  19.9 us (3%)
  between operations  13.8 us (2%)
    reduce_scatter x1, waiting for transfers between devices, body(): lax.psum_scatter(partial_t, 'pq', scatter_dimension=1, tiled=True)  279 us
    ppermute x7, waiting for transfers between devices, body(): lax.ppermute(ring[-1], 'pq', [(dev, (dev + 1) % 8) for dev in range(8)])  145 us
    psum x1, blocking collectives, body(): subspace = lax.psum(local_gram, ('pq', 'hh')) * factor  48.9 us
    unnamed x43, local copies, waits for them, and re-layouts  33.1 us
    all_gather x1, waiting for transfers between devices, body(): lax.all_gather(amplitudes, 'hh', axis=0, tiled=True)  25.3 us
    ppermute x7, starting transfers between devices, body(): lax.ppermute(ring[-1], 'pq', [(dev, (dev + 1) % 8) for dev in range(8)])  19.7 us
    dot_general x1, matrix products, body(): lax.dot_general(ladder_t, lax.all_gather(left_amps, 'hh', axis=1, tiled=T...  13.8 us
  transfers between devices with their start and end apart: 10, of which 9 were waited for; matrix products, arithmetic and copies ran while one was open for 5% of the time, Pallas kernels for 0%

profile of v1, /device:TPU:10, one launch (start us, length us, event | category | flops | bytes accessed | tf_op | source)
XLA Modules:
  0.0 596.2 jit_solution(3667333258902967755)
XLA Ops:
  7.2 0.0 copy-start
  7.2 0.0 all-gather.3.cloned.1.call-start
  7.2 0.7 all-gather.3.cloned.1.call-update
  7.9 0.0 reduce-scatter.2.cloned.1.call-start
  8.0 25.3 %all-gather.3.cloned.1.call-done = bf16[4096,256]{1,0:T(8,128)(2,1)} async-done(((bf16[1024,256]{1,0:T(8,128)(2,1)}), bf16[4096,256]{1,0:T(8,128)(2,1)}) %all-gather.3.cloned.1.call-update) | async-done | bytes 2097168 | tf_op jit(solution)/shard_map/all_gather | solution.py:15
  33.3 0.0 copy-done
  33.3 9.7 %fusion.14 = f32[1024,4096]{1,0:T(8,128)} fusion(bf16[1024,256]{1,0:T(8,128)(2,1)S(1)} %copy-done, bf16[4096,256]{1,0:T(8,128)(2,1)} %all-gather.3.cloned.1.call-done), kind=kOutput, calls=%fused_computation.26 | convolution fusion | flops 2147483648 | bytes 19398656 | tf_op jit(solution)/shard_map/dot_general | solution.py:13
  43.0 0.0 reduce-scatter.2.cloned.1.call-update
  43.0 0.0 all-gather.5.cloned.1.call-start
  43.0 0.7 all-gather.5.cloned.1.call-update
  43.7 278.6 %reduce-scatter.2.cloned.1.call-done = f32[1024,512]{1,0:T(8,128)} async-done(((f32[1024,4096]{1,0:T(8,128)}), f32[1024,512]{1,0:T(8,128)}) %reduce-scatter.2.cloned.1.call-update) | async-done | bytes 2097168 | tf_op jit(solution)/shard_map/reduce_scatter | solution.py:19
  322.3 0.0 copy-start.1
  322.3 1.9 convert_element_type.9
  324.2 1.7 collective-permute-start
  325.9 22.9 %collective-permute-done = bf16[1024,512]{1,0:T(8,128)(2,1)S(1)} collective-permute-done((bf16[1024,512]{1,0:T(8,128)(2,1)S(1)}, bf16[1024,512]{1,0:T(8,128)(2,1)S(1)}, u32[]{:S(2)}, u32[]{:S(2)}) %collective-permute-start) | collective-permute-done | bytes 1048608 | tf_op jit(solution)/shard_map/ppermute | solution.py:24
  348.8 0.0 copy-start.2
  348.8 1.0 copy-done.2
  349.7 2.9 collective-permute-start.1
  352.6 21.5 %collective-permute-done.1 = bf16[1024,512]{1,0:T(8,128)(2,1)S(1)} collective-permute-done((bf16[1024,512]{1,0:T(8,128)(2,1)S(1)}, bf16[1024,512]{1,0:T(8,128)(2,1)S(1)}, u32[]{:S(2)}, u32[]{:S(2)}) %collective-permute-start.1) | collective-permute-done | bytes 1048608 | tf_op jit(solution)/shard_map/ppermute | solution.py:24
  374.1 0.0 copy-start.4
  374.1 1.0 copy-done.4
  375.1 3.4 collective-permute-start.2
  378.5 20.8 %collective-permute-done.2 = bf16[1024,512]{1,0:T(8,128)(2,1)S(1)} collective-permute-done((bf16[1024,512]{1,0:T(8,128)(2,1)S(1)}, bf16[1024,512]{1,0:T(8,128)(2,1)S(1)}, u32[]{:S(2)}, u32[]{:S(2)}) %collective-permute-start.2) | collective-permute-done | bytes 1048608 | tf_op jit(solution)/shard_map/ppermute | solution.py:24
  399.3 1.0 copy-done.6
  400.3 3.3 collective-permute-start.3
  403.6 20.0 %collective-permute-done.3 = bf16[1024,512]{1,0:T(8,128)(2,1)S(1)} collective-permute-done((bf16[1024,512]{1,0:T(8,128)(2,1)S(1)}, bf16[1024,512]{1,0:T(8,128)(2,1)S(1)}, u32[]{:S(2)}, u32[]{:S(2)}) %collective-permute-start.3) | collective-permute-done | bytes 1048608 | tf_op jit(solution)/shard_map/ppermute | solution.py:24
  423.6 1.0 copy-done.8
  424.6 3.1 collective-permute-start.4
  427.7 19.6 %collective-permute-done.4 = bf16[1024,512]{1,0:T(8,128)(2,1)S(1)} collective-permute-done((bf16[1024,512]{1,0:T(8,128)(2,1)S(1)}, bf16[1024,512]{1,0:T(8,128)(2,1)S(1)}, u32[]{:S(2)}, u32[]{:S(2)}) %collective-permute-start.4) | collective-permute-done | bytes 1048608 | tf_op jit(solution)/shard_map/ppermute | solution.py:24
  447.3 1.0 copy-done.10
  448.3 2.8 collective-permute-start.5
  451.1 20.4 %collective-permute-done.5 = bf16[1024,512]{1,0:T(8,128)(2,1)} collective-permute-done((bf16[1024,512]{1,0:T(8,128)(2,1)S(1)}, bf16[1024,512]{1,0:T(8,128)(2,1)}, u32[]{:S(2)}, u32[]{:S(2)}) %collective-permute-start.5) | collective-permute-done | bytes 1048608 | tf_op jit(solution)/shard_map/ppermute | solution.py:24
  471.5 2.7 collective-permute-start.6
  474.2 0.0 copy-start.3
  474.2 19.8 %collective-permute-done.6 = bf16[1024,512]{1,0:T(8,128)(2,1)} collective-permute-done((bf16[1024,512]{1,0:T(8,128)(2,1)}, bf16[1024,512]{1,0:T(8,128)(2,1)}, u32[]{:S(2)}, u32[]{:S(2)}) %collective-permute-start.6) | collective-permute-done | bytes 1048608 | tf_op jit(solution)/shard_map/ppermute | solution.py:24
  494.0 2.3 constant_dynamic-update-slice_fusion.15
  496.3 2.3 constant_dynamic-update-slice_fusion.14
  498.7 2.3 constant_dynamic-update-slice_fusion.13
  501.0 2.3 constant_dynamic-update-slice_fusion.12
  503.3 2.3 constant_dynamic-update-slice_fusion.11
  505.6 2.3 constant_dynamic-update-slice_fusion.10
  507.9 2.3 constant_dynamic-update-slice_fusion.9
  510.2 0.0 copy-done.1
  510.2 1.1 constant_dynamic-update-slice_fusion.8
  511.3 2.3 constant_dynamic-update-slice_fusion.7
  513.6 2.3 constant_dynamic-update-slice_fusion.6
  515.9 0.0 copy-done.11
  515.9 1.1 constant_dynamic-update-slice_fusion.5
  517.0 0.0 copy-done.9
  517.0 1.0 constant_dynamic-update-slice_fusion.4
  518.0 0.0 copy-done.7
  518.0 1.1 constant_dynamic-update-slice_fusion.3
  519.1 0.0 copy-done.5
  519.1 1.1 constant_dynamic-update-slice_fusion.2
  520.2 0.0 copy-done.3
  520.2 1.1 constant_dynamic-update-slice_fusion.1
  521.3 1.2 constant_dynamic-update-slice_fusion
  522.4 13.8 %convert_bitcast_fusion = bf16[8,1024,128]{2,1,0:T(8,128)(2,1)S(1)} fusion(bf16[8,4096,128]{2,1,0:T(8,128)(2,1)} %all-gather.5.cloned.1.call-done, bf16[1024,8192]{1,0:T(8,128)(2,1)} %constant_dynamic-update-slice_fusion, s32[]{:T(128)S(6)} %select_n.14), kind=kOutput, calls=%fused_computation.6 | convolution fusion | flops 8590983168 | bytes 18874372 | tf_op jit(solution)/shard_map/dot_general | solution.py:28
  536.2 0.0 copy-start.13
  536.3 1.3 copy-done.13
  537.6 0.0 copy-done.12
  537.6 2.5 fusion.8
  540.1 48.9 %psum.7 = f32[8,8]{0,1:T(8,128)S(1)} all-reduce(f32[8,8]{0,1:T(8,128)S(1)} %fusion.8), channel_id=1, replica_groups=mesh['pq'=8,'hh'=4] {'pq','hh'}, use_global_device_ids=true, to_apply=%region_1.2 | all-reduce | flops 64 | bytes 512 | tf_op jit(solution)/shard_map/psum | solution.py:41
  589.0 0.7 copy.7
  (10 shorter events, 0.0 us)
Async XLA Ops:
  7.2 26.1 %copy-start = (bf16[1024,256]{1,0:T(8,128)(2,1)S(1)}, bf16[1024,256]{1,0:T(8,128)(2,1)}, u32[]{:S(2)}) copy-start(bf16[1024,256]{1,0:T(8,128)(2,1)} %param.4) | copy-start | bytes 1572868
  7.2 26.1 %all-gather.3.cloned.1.call-start = ((), (), s32[]{:S(2)}) async-start(), calls=%async_computation.1 | async-start | bytes 2621440 | tf_op jit(solution)/shard_map/all_gather | solution.py:15
  7.9 314.4 %reduce-scatter.2.cloned.1.call-start = ((), (), s32[]{:S(2)}) async-start(), calls=%async_computation.2 | async-start | bytes 18874368 | tf_op jit(solution)/shard_map/reduce_scatter | solution.py:19
  43.0 479.4 %all-gather.5.cloned.1.call-start = ((), (), s32[]{:S(2)}) async-start(), calls=%async_computation.3 | async-start | bytes 10485760 | tf_op jit(solution)/shard_map/all_gather | solution.py:30
  322.3 187.9 %copy-start.1 = (f32[1024,512]{1,0:T(8,128)S(1)}, f32[1024,512]{1,0:T(8,128)}, u32[]{:S(2)}) copy-start(f32[1024,512]{1,0:T(8,128)} %reduce-scatter.2.cloned.1.call-done) | copy-start | bytes 6291460
  324.2 24.6 %collective-permute-start = (bf16[1024,512]{1,0:T(8,128)(2,1)S(1)}, bf16[1024,512]{1,0:T(8,128)(2,1)S(1)}, u32[]{:S(2)}, u32[]{:S(2)}) collective-permute-start(bf16[1024,512]{1,0:T(8,128)(2,1)S(1)} %convert_element_type.9), channel_id=1, source_target_pairs={{0,4},{4,8},{8,12},{12,16},{16,20},{20,24},{24,28},{28,0},{1,5},{5... | collective-permute-start | bytes 3145736 | tf_op jit(solution)/shard_map/ppermute | solution.py:24
  348.8 1.0 copy-start.2
  349.7 24.4 %collective-permute-start.1 = (bf16[1024,512]{1,0:T(8,128)(2,1)S(1)}, bf16[1024,512]{1,0:T(8,128)(2,1)S(1)}, u32[]{:S(2)}, u32[]{:S(2)}) collective-permute-start(bf16[1024,512]{1,0:T(8,128)(2,1)S(1)} %collective-permute-done), channel_id=1, source_target_pairs={{0,4},{4,8},{8,12},{12,16},{16,20},{20,24},{24,28},{28,0},{1,5},{5... | collective-permute-start | bytes 3145736 | tf_op jit(solution)/shard_map/ppermute | solution.py:24
  374.1 1.0 copy-start.4
  375.1 24.1 %collective-permute-start.2 = (bf16[1024,512]{1,0:T(8,128)(2,1)S(1)}, bf16[1024,512]{1,0:T(8,128)(2,1)S(1)}, u32[]{:S(2)}, u32[]{:S(2)}) collective-permute-start(bf16[1024,512]{1,0:T(8,128)(2,1)S(1)} %collective-permute-done.1), channel_id=1, source_target_pairs={{0,4},{4,8},{8,12},{12,16},{16,20},{20,24},{24,28},{28,0},{1,5},{5... | collective-permute-start | bytes 3145736 | tf_op jit(solution)/shard_map/ppermute | solution.py:24
  399.3 1.0 copy-start.6
  400.3 23.3 %collective-permute-start.3 = (bf16[1024,512]{1,0:T(8,128)(2,1)S(1)}, bf16[1024,512]{1,0:T(8,128)(2,1)S(1)}, u32[]{:S(2)}, u32[]{:S(2)}) collective-permute-start(bf16[1024,512]{1,0:T(8,128)(2,1)S(1)} %collective-permute-done.2), channel_id=1, source_target_pairs={{0,4},{4,8},{8,12},{12,16},{16,20},{20,24},{24,28},{28,0},{1,5},{5... | collective-permute-start | bytes 3145736 | tf_op jit(solution)/shard_map/ppermute | solution.py:24
  423.6 1.0 copy-start.8
  424.6 22.7 %collective-permute-start.4 = (bf16[1024,512]{1,0:T(8,128)(2,1)S(1)}, bf16[1024,512]{1,0:T(8,128)(2,1)S(1)}, u32[]{:S(2)}, u32[]{:S(2)}) collective-permute-start(bf16[1024,512]{1,0:T(8,128)(2,1)S(1)} %collective-permute-done.3), channel_id=1, source_target_pairs={{0,4},{4,8},{8,12},{12,16},{16,20},{20,24},{24,28},{28,0},{1,5},{5... | collective-permute-start | bytes 3145736 | tf_op jit(solution)/shard_map/ppermute | solution.py:24
  447.3 1.0 copy-start.10
  448.3 23.2 %collective-permute-start.5 = (bf16[1024,512]{1,0:T(8,128)(2,1)S(1)}, bf16[1024,512]{1,0:T(8,128)(2,1)}, u32[]{:S(2)}, u32[]{:S(2)}) collective-permute-start(bf16[1024,512]{1,0:T(8,128)(2,1)S(1)} %collective-permute-done.4), channel_id=1, source_target_pairs={{0,4},{4,8},{8,12},{12,16},{16,20},{20,24},{24,28},{28,0},{1,5},{5... | collective-permute-start | bytes 3145736 | tf_op jit(solution)/shard_map/ppermute | solution.py:24
  471.5 22.5 %collective-permute-start.6 = (bf16[1024,512]{1,0:T(8,128)(2,1)}, bf16[1024,512]{1,0:T(8,128)(2,1)}, u32[]{:S(2)}, u32[]{:S(2)}) collective-permute-start(bf16[1024,512]{1,0:T(8,128)(2,1)} %collective-permute-done.5), channel_id=1, source_target_pairs={{0,4},{4,8},{8,12},{12,16},{16,20},{20,24},{24,28},{28,0},{1,5},{5... | collective-permute-start | bytes 3145736 | tf_op jit(solution)/shard_map/ppermute | solution.py:24
  474.2 41.7 %copy-start.11 = (bf16[1024,512]{1,0:T(8,128)(2,1)S(1)}, bf16[1024,512]{1,0:T(8,128)(2,1)}, u32[]{:S(2)}) copy-start(bf16[1024,512]{1,0:T(8,128)(2,1)} %copy-done.10) | copy-start | bytes 3145732
  474.2 42.8 %copy-start.9 = (bf16[1024,512]{1,0:T(8,128)(2,1)S(1)}, bf16[1024,512]{1,0:T(8,128)(2,1)}, u32[]{:S(2)}) copy-start(bf16[1024,512]{1,0:T(8,128)(2,1)} %copy-done.8) | copy-start | bytes 3145732
  474.2 43.9 %copy-start.7 = (bf16[1024,512]{1,0:T(8,128)(2,1)S(1)}, bf16[1024,512]{1,0:T(8,128)(2,1)}, u32[]{:S(2)}) copy-start(bf16[1024,512]{1,0:T(8,128)(2,1)} %copy-done.6) | copy-start | bytes 3145732
  474.2 44.9 %copy-start.5 = (bf16[1024,512]{1,0:T(8,128)(2,1)S(1)}, bf16[1024,512]{1,0:T(8,128)(2,1)}, u32[]{:S(2)}) copy-start(bf16[1024,512]{1,0:T(8,128)(2,1)} %copy-done.4) | copy-start | bytes 3145732
  474.2 46.0 %copy-start.3 = (bf16[1024,512]{1,0:T(8,128)(2,1)S(1)}, bf16[1024,512]{1,0:T(8,128)(2,1)}, u32[]{:S(2)}) copy-start(bf16[1024,512]{1,0:T(8,128)(2,1)} %copy-done.2) | copy-start | bytes 3145732
  522.4 15.1 %copy-start.12 = (bf16[8,1024,128]{2,1,0:T(8,128)(2,1)S(1)}, bf16[8,1024,128]{2,1,0:T(8,128)(2,1)}, u32[]{:S(2)}) copy-start(bf16[8,1024,128]{2,1,0:T(8,128)(2,1)} %param.5) | copy-start | bytes 6291460
  536.2 1.3 copy-start.13
Sparse Core Ops, SparseCore 0:
  9.5 23.6 all-gather.2
  43.1 279.1 reduce-scatter.1
  323.9 58.3 all-gather.4
